TPU v7x, 32 devices: a whole 2x2x4 slice. The times are simulated.
32 devices in a mesh: feat: 8 (over z, y), samp: 4 (over x, core).
Axes of the slice: x: 2, y: 2, z: 4, core: 2. Of those that a mesh axis runs over, the one named last changes fastest.
Arguments:
- design: bfloat16 [14336, 8192], P('samp', 'feat'), may hold values from -0.0625 to 0.0625
- targets: bfloat16 [14336, 128], P('samp'), may hold values from -26 to 26
- warm_start: float32 [8192, 128], P('feat'), may hold values from -0.6 to 0.6
- active_mask: int32 [2, 8192], P(None, 'feat'), may hold values 0 or 1
- penalty_index: int32 [1], replicated, may hold values from 0 to 7
Outputs:
- coefficients: float32 [8192, 128], P('feat')
- correlations: float32 [3, 8192], P(None, 'feat')
- relative_gaps: float32 [3], replicated
- pruned_counts: float32 [2], replicated
All inputs are finite; a program needn't handle non-finite values. No bound on the sum of `active_mask` on one device may be relied on, other than what follows from the above.
Results may differ from a plain program's by a relative error of at most 0.0024.
The roundings to bfloat16 on the way count: a program that leaves them out, or rounds other values in their place, can miss the bound.
Values may be sent and summed in bfloat16 or wider, within the bound.
A program may use at most 64 MiB of HBM per device.

v0:
```python
import jax
import jax.numpy as jnp
from jax import lax
from jax.sharding import PartitionSpec as P

ITERS = 2


def group_norms(matrix):
    return jnp.sqrt(jnp.sum(matrix * matrix, axis=1))


def transpose_product(design, right_side):
    return lax.dot_general(
        design, right_side, (((0,), (0,)), ((), ())), preferred_element_type=jnp.float32
    )


def local(design, targets, warm_start, active_mask, penalty_index):
    row_count, col_count = design.shape
    feat_size = lax.axis_size("feat")
    feat_slot = lax.axis_index("feat")
    block_rows = row_count // feat_size
    samp_first = (lax.axis_index("samp") == 0).astype(jnp.float32)
    corr_local = transpose_product(design, targets)
    squares_local = jnp.sum(jnp.square(design.astype(jnp.float32)), axis=0)
    corr_y, column_squares = lax.psum((corr_local, squares_local), "samp")
    penalty_max = lax.pmax(jnp.max(group_norms(corr_y)), "feat")
    penalty = penalty_max / (8.0 + 4.0 * penalty_index[0].astype(jnp.float32))
    step_sizes = 0.5 / (1.0 + column_squares)
    current = warm_start
    correlations = []
    relative_gaps = []
    pruned_counts = []
    own_targets = lax.dynamic_slice_in_dim(targets, feat_slot * block_rows, block_rows, 0)
    for iteration in range(ITERS + 1):
        current_half = current.astype(jnp.bfloat16)
        fitted_part = jnp.dot(design, current_half, preferred_element_type=jnp.float32)
        fitted = lax.psum(fitted_part, "feat")
        residual_all = (targets.astype(jnp.float32) - fitted).astype(jnp.bfloat16)
        residual = lax.dynamic_slice_in_dim(residual_all, feat_slot * block_rows, block_rows, 0)
        grad_local = transpose_product(design, residual_all)
        resid_float = residual.astype(jnp.float32)
        rr_local = jnp.sum(resid_float * resid_float)
        ry_local = jnp.sum(resid_float * own_targets.astype(jnp.float32))
        bn_local = samp_first * jnp.sum(group_norms(current))
        if iteration < ITERS:
            keep = active_mask[iteration].astype(jnp.float32)
            pruned_local = samp_first * jnp.sum(1.0 - keep)
        else:
            pruned_local = jnp.zeros((), jnp.float32)
        gradient = lax.psum(grad_local, "samp")
        grad_norms = group_norms(gradient)
        local_max = jnp.max(grad_norms)
        grad_top = lax.pmax(local_max, "feat")
        rr_sum, ry_sum, bn_sum, pruned_sum = lax.psum(
            (rr_local, ry_local, bn_local, pruned_local), ("feat", "samp")
        )
        scale = jnp.maximum(penalty, grad_top)
        correlations.append(grad_norms / scale)
        primal = 0.5 * rr_sum + penalty * bn_sum
        ratio = penalty / scale
        dual = ratio * ry_sum - 0.5 * ratio * ratio * rr_sum
        relative_gaps.append((primal - dual) / (primal + 1.0))
        if iteration < ITERS:
            pruned_counts.append(pruned_sum)
            moved = current + step_sizes[:, None] * gradient
            moved_norms = group_norms(moved)
            cutoff = step_sizes * penalty
            factor = jnp.maximum(moved_norms - cutoff, 0.0) / jnp.maximum(moved_norms, cutoff)
            current = (keep * factor)[:, None] * moved
    return (current, jnp.stack(correlations), jnp.stack(relative_gaps), jnp.stack(pruned_counts))


def solution(mesh):
    placed = (P("samp", "feat"), P("samp", None), P("feat", None), P(None, "feat"), P())
    return jax.shard_map(
        local,
        mesh=mesh,
        in_specs=placed,
        out_specs=(P("feat", None), P(None, "feat"), P(), P()),
        check_vma=False,
    )
```

profile of v0, /device:TPU:0, one launch (start us, length us, event | category | flops | bytes accessed | tf_op | source)
XLA Modules:
  0.0 527.3 jit_solution(8647449387170644454)
XLA Ops:
  7.2 6.5 %fusion.5 = f32[3584,128]{1,0:T(8,128)} fusion(bf16[3584,1024]{1,0:T(8,128)(2,1)} %param.5, f32[1024,128]{1,0:T(8,128)} %param.7), kind=kOutput, calls=%fused_computation.33 | convolution fusion | flops 939655168 | bytes 9699328 | tf_op jit(solution)/shard_map/dot_general | solution.py:38
  13.8 6.0 %fusion.13 = f32[1024,128]{1,0:T(8,128)} fusion(bf16[3584,1024]{1,0:T(8,128)(2,1)} %param.5, bf16[3584,128]{1,0:T(8,128)(2,1)S(1)} %copy-done), kind=kOutput, calls=%fused_computation.61 | convolution fusion | flops 939524096 | bytes 8781824 | tf_op jit(solution)/shard_map/dot_general | solution.py:14
  19.8 92.7 %all-reduce.10.cloned.1.call-done = f32[3584,128]{1,0:T(8,128)} async-done(((f32[3584,128]{1,0:T(8,128)}), f32[3584,128]{1,0:T(8,128)}) %all-reduce.10.cloned.1.call-update) | async-done | bytes 1835024 | tf_op jit(solution)/shard_map/psum | solution.py:39
  112.5 1.7 fusion
  114.1 5.0 convolution_bitcast_fusion.4
  119.3 4.6 multiply_reduce_fusion
  123.9 1.0 copy.9
  125.5 7.1 %psum.133 = f32[1024]{0:T(1024)S(1)} all-reduce(f32[1024]{0:T(1024)S(1)} %multiply_reduce_fusion), channel_id=1, replica_groups=mesh['feat'=8,'samp'=4] {'samp'}, use_global_device_ids=true, to_apply=%region_1.0 | all-reduce | flops 1024 | bytes 8192 | tf_op jit(solution)/shard_map/psum | solution.py:27
  132.7 22.5 %all-reduce.20.cloned.1.call-done = (f32[1024,128]{0,1:T(8,128)}, f32[1024,128]{1,0:T(8,128)}) async-done(((f32[1024,128]{0,1:T(8,128)}, f32[1024,128]{1,0:T(8,128)}), (f32[1024,128]{0,1:T(8,128)}, f32[1024,128]{1,0:T(8,128)})) %all-reduce.20.cloned.1.call-update) | async-done | bytes 1048592 | tf_op jit(solution)/shard_map/psum | solution.py:52
  155.2 1.2 multiply_reduce_fusion.8
  157.1 22.0 %pmax.28 = f32[]{:T(128)} all-reduce(f32[]{:T(128)} %sqrt_reduce_fusion.3), channel_id=1, replica_groups=mesh['feat'=8,'samp'=4] {'feat'}, use_global_device_ids=true, to_apply=%region_8.0 | all-reduce | flops 1 | bytes 8 | tf_op jit(solution)/shard_map/pmax | solution.py:28
  179.7 1.3 multiply_reduce_fusion.9
  181.7 6.4 %convolution_bitcast_fusion.1 = f32[3584,128]{1,0:T(8,128)} fusion(bf16[3584,1024]{1,0:T(8,128)(2,1)} %param.5, f32[1024,128]{0,1:T(8,128)S(1)} %get-tuple-element.36, f32[1024]{0:T(1024)S(1)} %get-tuple-element.41), kind=kOutput, calls=%fused_computation.2 | convolution fusion | flops 939786240 | bytes 9703424 | tf_op jit(solution)/shard_map/dot_general | solution.py:38
  188.1 92.7 %all-reduce.12.cloned.1.call-done = f32[3584,128]{1,0:T(8,128)} async-done(((f32[3584,128]{1,0:T(8,128)}), f32[3584,128]{1,0:T(8,128)}) %all-reduce.12.cloned.1.call-update) | async-done | bytes 1835024 | tf_op jit(solution)/shard_map/psum | solution.py:39
  280.9 1.7 fusion.1
  282.6 5.0 convolution_bitcast_fusion.3
  287.8 32.8 %all-reduce.14.cloned.1.call-done = f32[1024,128]{0,1:T(8,128)} async-done(((f32[1024,128]{0,1:T(8,128)}), f32[1024,128]{0,1:T(8,128)}) %all-reduce.14.cloned.1.call-update) | async-done | bytes 524304 | tf_op jit(solution)/shard_map/psum | solution.py:52
  320.7 1.2 multiply_reduce_fusion.2
  322.6 1.2 multiply_reduce_fusion.1
  323.8 0.8 copy-done.2
  324.5 6.4 %convolution_bitcast_fusion = f32[3584,128]{1,0:T(8,128)} fusion(bf16[3584,1024]{1,0:T(8,128)(2,1)} %param.5, f32[1024,128]{0,1:T(8,128)S(1)} %get-tuple-element.34), kind=kOutput, calls=%fused_computation.1 | convolution fusion | flops 939655168 | bytes 9699328 | tf_op jit(solution)/shard_map/dot_general | solution.py:38
  334.3 92.8 %all-reduce.16.cloned.1.call-done = f32[3584,128]{1,0:T(8,128)} async-done(((f32[3584,128]{1,0:T(8,128)}), f32[3584,128]{1,0:T(8,128)}) %all-reduce.16.cloned.1.call-update) | async-done | bytes 1835024 | tf_op jit(solution)/shard_map/psum | solution.py:39
  427.1 1.7 fusion.2
  428.7 0.9 copy-done.1
  429.7 5.1 convolution_bitcast_fusion.2
  435.4 1.0 copy.12
  439.0 1.7 fusion.10
  440.7 41.8 %all-reduce = (f32[]{:T(128)}, f32[]{:T(128)}, f32[]{:T(128)}, f32[]{:T(128)}, f32[]{:T(128)}, /*index=5*/f32[]{:T(128)}, f32[]{:T(128)}, f32[]{:T(128)}, f32[]{:T(128)}, f32[1]{0:T(128)}, /*index=10*/f32[1]{0:T(128)}) all-reduce(f32[]{:T(128)} %get-tuple-element.12, ...), channel_id=1, replica_groups=mesh['feat'=8,'samp'=4] {'feat','samp'}, use_global_device_ids=true, to_apply=%region_38.0 | all-reduce | flops 11 | bytes 88 | tf_op jit(solution)/shard_map/psum | solution.py:56
  486.2 1.9 pad_maximum_fusion.2
  488.1 1.1 multiply_reduce_fusion.4
  489.2 0.7 sqrt_reduce_fusion.4
  489.9 21.7 %all-reduce.1 = (f32[]{:T(128)}, f32[]{:T(128)}, f32[]{:T(128)}) all-reduce(f32[]{:T(128)} %sqrt_reduce_fusion.4, f32[]{:T(128)} %sqrt_reduce_fusion.5, f32[]{:T(128)} %sqrt_reduce_fusion.6), channel_id=1, replica_groups=mesh['feat'=8,'samp'=4] {'feat'}, use_global_device_ids=true, to_apply=%region_22.0 | all-reduce | flops 3 | bytes 24 | tf_op jit(solution)/shard_map/pmax | solution.py:55
  (41 shorter events, 6.9 us)
Async XLA Ops:
  7.2 6.6 %copy-start = (bf16[3584,128]{1,0:T(8,128)(2,1)S(1)}, bf16[3584,128]{1,0:T(8,128)(2,1)}, u32[]{:S(2)}) copy-start(bf16[3584,128]{1,0:T(8,128)(2,1)} %param.6) | copy-start | bytes 2752516
  7.2 105.3 %all-reduce.10.cloned.1.call-start = ((), (), s32[]{:S(2)}) async-start(), calls=%async_computation | async-start | bytes 3670016 | tf_op jit(solution)/shard_map/psum | solution.py:39
  13.7 141.5 %all-reduce.20.cloned.1.call-start = ((), (), s32[]{:S(2)}) async-start(), calls=%async_computation.5 | async-start | bytes 2097152 | tf_op jit(solution)/shard_map/psum | solution.py:52
  119.2 4.7 copy-start.4
  119.2 13.5 %copy-start.6 = (s32[2,1024]{1,0:T(2,128)S(1)}, s32[2,1024]{1,0:T(2,128)}, u32[]{:S(2)}) copy-start(s32[2,1024]{1,0:T(2,128)} %param.8) | copy-start | bytes 24580
  119.2 161.7 %all-reduce.12.cloned.1.call-start = ((), (), s32[]{:S(2)}) async-start(), calls=%async_computation.1 | async-start | bytes 3670016 | tf_op jit(solution)/shard_map/psum | solution.py:39
  188.1 132.6 %all-reduce.14.cloned.1.call-start = ((), (), s32[]{:S(2)}) async-start(), calls=%async_computation.2 | async-start | bytes 1048576 | tf_op jit(solution)/shard_map/psum | solution.py:52
  287.6 139.5 %all-reduce.16.cloned.1.call-start = ((), (), s32[]{:S(2)}) async-start(), calls=%async_computation.3 | async-start | bytes 3670016 | tf_op jit(solution)/shard_map/psum | solution.py:39
  323.7 0.8 copy-start.2
  323.8 7.3 %copy-start.5 = (f32[1024,128]{1,0:T(8,128)S(1)}, f32[1024,128]{1,0:T(8,128)}, u32[]{:S(2)}) copy-start(f32[1024,128]{1,0:T(8,128)} %param.7) | copy-start | bytes 1572868
  331.0 157.1 %all-reduce.18.cloned.1.call-start = ((), (), s32[]{:S(2)}) async-start(), calls=%async_computation.4 | async-start | bytes 1048576 | tf_op jit(solution)/shard_map/psum | solution.py:52
  428.7 0.9 copy-start.1
  429.7 5.8 %copy-start.3 = (f32[1024,128]{0,1:T(8,128)S(1)}, f32[1024,128]{0,1:T(8,128)}, u32[]{:S(2)}) copy-start(f32[1024,128]{0,1:T(8,128)} %copy-done.2) | copy-start | bytes 1572868
Sparse Core Ops, SparseCore 0:
  13.9 98.5 all-reduce.9
  119.3 35.8 all-reduce.19
  188.2 92.6 all-reduce.11
  287.7 32.9 all-reduce.13
  331.1 95.9 all-reduce.15
  434.9 33.1 all-reduce.17
where the time goes:
time: 528 us; the launch traced here: 527 us
  waiting for transfers between devices  334 us (63%)
  blocking collectives  92.5 us (18%)
  matrix products  40.5 us (8%)
  between operations  30.1 us (6%)
  other arithmetic  26.4 us (5%)
    psum x3, waiting for transfers between devices, local(): fitted = lax.psum(fitted_part, 'feat')  278 us
    psum x3, waiting for transfers between devices, local(): gradient = lax.psum(grad_local, 'samp')  55.4 us
    psum x1, blocking collectives, local(): lax.psum((rr_local, ry_local, bn_local, pruned_local), ('feat', 'samp'))  41.8 us
    pmax x1, blocking collectives, local(): penalty_max = lax.pmax(jnp.max(group_norms(corr_y)), 'feat')  22 us
    pmax x1, blocking collectives, local(): grad_top = lax.pmax(local_max, 'feat')  21.7 us
    dot_general x4, matrix products, transpose_product(): lax.dot_general(design, right_side, (((0,), (0,)), ((), ())), preferred_e...  21.2 us
    dot_general x3, matrix products, local(): jnp.dot(design, current_half, preferred_element_type=jnp.float32)  19.3 us
  transfers between devices with their start and end apart: 6, of which 5 were waited for; matrix products, arithmetic and copies ran while one was open for 4% of the time, Pallas kernels for 0%

commit v1 on v0

--- a/solution.py
+++ b/solution.py
@@ -36,7 +36,9 @@
     for iteration in range(ITERS + 1):
         current_half = current.astype(jnp.bfloat16)
         fitted_part = jnp.dot(design, current_half, preferred_element_type=jnp.float32)
-        fitted = lax.psum(fitted_part, "feat")
+        fitted = fitted_part
+        for hop in (1, 2, 4):
+            fitted = fitted + lax.ppermute(fitted, "feat", [(dev, dev ^ hop) for dev in range(8)])
         residual_all = (targets.astype(jnp.float32) - fitted).astype(jnp.bfloat16)
         residual = lax.dynamic_slice_in_dim(residual_all, feat_slot * block_rows, block_rows, 0)
         grad_local = transpose_product(design, residual_all)

time: 528 us -> 706 us (1.34)
  waiting for transfers between devices: 334 us -> 512 us
  starting transfers between devices: 0.43 us -> 13.8 us
  matrix products: 40.5 us -> 28 us
    ppermute x0 -> x9, waiting for transfers between devices: none -> 455 us  [local(): lax.ppermute(fitted, 'feat', [(dev, dev ^ hop) for dev in range(8)])]
    psum x3 -> x0, waiting for transfers between devices: 278 us -> none  [local(): fitted = lax.psum(fitted_part, 'feat')]
    ppermute x0 -> x9, starting transfers between devices: none -> 13.7 us  [local(): lax.ppermute(fitted, 'feat', [(dev, dev ^ hop) for dev in range(8)])]
    dot_general x4, matrix products: 21.2 us -> 12 us  [transpose_product(): lax.dot_general(design, right_side, (((0,), (0,)), ((), ())), preferred_e...]
  transfers between devices with their start and end apart: 6 -> 12, of which waited for: 5 -> 11; matrix products, arithmetic and copies ran while one was open for 4% -> 2% of each run, Pallas kernels for 0% -> 0%
where the time goes in v1:
time: 706 us; the launch traced here: 705 us
  waiting for transfers between devices  512 us (73%)
  blocking collectives  91.6 us (13%)
  between operations  29.8 us (4%)
  matrix products  28 us (4%)
  other arithmetic  26.7 us (4%)
  starting transfers between devices  13.8 us (2%)
    ppermute x9, waiting for transfers between devices, local(): lax.ppermute(fitted, 'feat', [(dev, dev ^ hop) for dev in range(8)])  455 us
    psum x3, waiting for transfers between devices, local(): gradient = lax.psum(grad_local, 'samp')  56.2 us
    psum x1, blocking collectives, local(): lax.psum((rr_local, ry_local, bn_local, pruned_local), ('feat', 'samp'))  41.7 us
    pmax x1, blocking collectives, local(): penalty_max = lax.pmax(jnp.max(group_norms(corr_y)), 'feat')  22.2 us
    pmax x1, blocking collectives, local(): grad_top = lax.pmax(local_max, 'feat')  21.3 us
    dot_general x3, matrix products, local(): jnp.dot(design, current_half, preferred_element_type=jnp.float32)  16 us
  transfers between devices with their start and end apart: 12, of which 11 were waited for; matrix products, arithmetic and copies ran while one was open for 2% of the time, Pallas kernels for 0%

profile of v1, /device:TPU:0, one launch (start us, length us, event | category | flops | bytes accessed | tf_op | source)
XLA Modules:
  0.0 704.7 jit_solution(10835733695531140306)
XLA Ops:
  7.2 5.4 fusion.5
  12.6 3.1 collective-permute-start
  15.7 40.0 %collective-permute-done = f32[3584,128]{1,0:T(8,128)S(1)} collective-permute-done((f32[3584,128]{1,0:T(8,128)S(1)}, f32[3584,128]{1,0:T(8,128)S(1)}, u32[]{:S(2)}, u32[]{:S(2)}) %collective-permute-start) | collective-permute-done | bytes 1835040 | tf_op jit(solution)/shard_map/ppermute | solution.py:41
  55.9 1.9 collective-permute-start.1
  57.8 39.4 %collective-permute-done.1 = f32[3584,128]{1,0:T(8,128)S(1)} collective-permute-done((f32[3584,128]{1,0:T(8,128)S(1)}, f32[3584,128]{1,0:T(8,128)S(1)}, u32[]{:S(2)}, u32[]{:S(2)}) %collective-permute-start.1) | collective-permute-done | bytes 1835040 | tf_op jit(solution)/shard_map/ppermute | solution.py:41
  97.4 2.6 collective-permute-start.2
  100.0 2.9 fusion.13
  102.9 75.1 %collective-permute-done.2 = f32[3584,128]{1,0:T(8,128)S(1)} collective-permute-done((f32[3584,128]{1,0:T(8,128)S(1)}, f32[3584,128]{1,0:T(8,128)S(1)}, u32[]{:S(2)}, u32[]{:S(2)}) %collective-permute-start.2) | collective-permute-done | bytes 1835040 | tf_op jit(solution)/shard_map/ppermute | solution.py:41
  178.3 2.0 convolution_bitcast_fusion.4
  180.4 4.6 multiply_reduce_fusion
  186.7 6.4 psum.112
  193.1 24.5 %all-reduce.11.cloned.1.call-done = (f32[1024,128]{0,1:T(8,128)}, f32[1024,128]{1,0:T(8,128)}) async-done(((f32[1024,128]{0,1:T(8,128)}, f32[1024,128]{1,0:T(8,128)}), (f32[1024,128]{0,1:T(8,128)}, f32[1024,128]{1,0:T(8,128)})) %all-reduce.11.cloned.1.call-update) | async-done | bytes 1048592 | tf_op jit(solution)/shard_map/psum | solution.py:54
  219.5 22.2 %pmax.28 = f32[]{:T(128)} all-reduce(f32[]{:T(128)} %sqrt_reduce_fusion.3), channel_id=1, replica_groups=mesh['feat'=8,'samp'=4] {'feat'}, use_global_device_ids=true, to_apply=%region_7.0 | all-reduce | flops 1 | bytes 8 | tf_op jit(solution)/shard_map/pmax | solution.py:28
  244.3 5.2 convolution_bitcast_fusion.1
  249.6 37.4 %collective-permute-done.3 = f32[3584,128]{1,0:T(8,128)S(1)} collective-permute-done((f32[3584,128]{1,0:T(8,128)S(1)}, f32[3584,128]{1,0:T(8,128)S(1)}, u32[]{:S(2)}, u32[]{:S(2)}) %collective-permute-start.3) | collective-permute-done | bytes 1835040 | tf_op jit(solution)/shard_map/ppermute | solution.py:41
  287.3 37.7 %collective-permute-done.4 = f32[3584,128]{1,0:T(8,128)S(1)} collective-permute-done((f32[3584,128]{1,0:T(8,128)S(1)}, f32[3584,128]{1,0:T(8,128)S(1)}, u32[]{:S(2)}, u32[]{:S(2)}) %collective-permute-start.4) | collective-permute-done | bytes 1835040 | tf_op jit(solution)/shard_map/ppermute | solution.py:41
  325.3 74.8 %collective-permute-done.5 = f32[3584,128]{1,0:T(8,128)S(1)} collective-permute-done((f32[3584,128]{1,0:T(8,128)S(1)}, f32[3584,128]{1,0:T(8,128)S(1)}, u32[]{:S(2)}, u32[]{:S(2)}) %collective-permute-start.5) | collective-permute-done | bytes 1835040 | tf_op jit(solution)/shard_map/ppermute | solution.py:41
  400.4 2.0 convolution_bitcast_fusion.3
  402.5 31.7 %all-reduce.7.cloned.1.call-done = f32[1024,128]{0,1:T(8,128)} async-done(((f32[1024,128]{0,1:T(8,128)}), f32[1024,128]{0,1:T(8,128)}) %all-reduce.7.cloned.1.call-update) | async-done | bytes 524304 | tf_op jit(solution)/shard_map/psum | solution.py:54
  437.2 5.4 convolution_bitcast_fusion
  442.6 1.5 collective-permute-start.6
  444.2 39.1 %collective-permute-done.6 = f32[3584,128]{1,0:T(8,128)S(1)} collective-permute-done((f32[3584,128]{1,0:T(8,128)S(1)}, f32[3584,128]{1,0:T(8,128)S(1)}, u32[]{:S(2)}, u32[]{:S(2)}) %collective-permute-start.6) | collective-permute-done | bytes 1835040 | tf_op jit(solution)/shard_map/ppermute | solution.py:41
  483.5 1.8 collective-permute-start.7
  485.3 38.2 %collective-permute-done.7 = f32[3584,128]{1,0:T(8,128)S(1)} collective-permute-done((f32[3584,128]{1,0:T(8,128)S(1)}, f32[3584,128]{1,0:T(8,128)S(1)}, u32[]{:S(2)}, u32[]{:S(2)}) %collective-permute-start.7) | collective-permute-done | bytes 1835040 | tf_op jit(solution)/shard_map/ppermute | solution.py:41
  524.9 2.7 collective-permute-start.8
  530.8 73.7 %collective-permute-done.8 = f32[3584,128]{1,0:T(8,128)} collective-permute-done((f32[3584,128]{1,0:T(8,128)}, f32[3584,128]{1,0:T(8,128)}, u32[]{:S(2)}, u32[]{:S(2)}) %collective-permute-start.8) | collective-permute-done | bytes 1835040 | tf_op jit(solution)/shard_map/ppermute | solution.py:41
  604.6 2.3 fusion.2
  607.8 5.1 convolution_bitcast_fusion.2
  617.1 1.7 fusion.10
  618.8 41.7 %all-reduce = (f32[]{:T(128)}, f32[]{:T(128)}, f32[]{:T(128)}, f32[]{:T(128)}, f32[]{:T(128)}, /*index=5*/f32[]{:T(128)}, f32[]{:T(128)}, f32[]{:T(128)}, f32[]{:T(128)}, f32[1]{0:T(128)}, /*index=10*/f32[1]{0:T(128)}) all-reduce(f32[]{:T(128)} %get-tuple-element.12, ...), channel_id=1, replica_groups=mesh['feat'=8,'samp'=4] {'feat','samp'}, use_global_device_ids=true, to_apply=%region_35.0 | all-reduce | flops 11 | bytes 88 | tf_op jit(solution)/shard_map/psum | solution.py:58
  664.3 1.9 pad_maximum_fusion.2
  667.9 21.3 %all-reduce.1 = (f32[]{:T(128)}, f32[]{:T(128)}, f32[]{:T(128)}) all-reduce(f32[]{:T(128)} %sqrt_reduce_fusion.4, f32[]{:T(128)} %sqrt_reduce_fusion.5, f32[]{:T(128)} %sqrt_reduce_fusion.6), channel_id=1, replica_groups=mesh['feat'=8,'samp'=4] {'feat'}, use_global_device_ids=true, to_apply=%region_19.0 | all-reduce | flops 3 | bytes 24 | tf_op jit(solution)/shard_map/pmax | solution.py:57
  (66 shorter events, 19.5 us)
Async XLA Ops:
  7.2 210.5 %all-reduce.11.cloned.1.call-start = ((), (), s32[]{:S(2)}) async-start(), calls=%async_computation.2 | async-start | bytes 2097152 | tf_op jit(solution)/shard_map/psum | solution.py:54
  7.2 92.8 %slice-start = ((s8[7340032]{0:T(1024)(128)(4,1)}), s8[4194304]{0:T(1024)(128)(4,1)S(1)}, s32[]{:S(2)}) async-start(s8[7340032]{0:T(1024)(128)(4,1)} %bitcast.32), calls=%async_computation.3 | async-start | bytes 8388608
  12.6 87.4 %slice-start.1 = ((s8[7340032]{0:T(1024)(128)(4,1)}), s8[3145728]{0:T(1024)(128)(4,1)S(1)}, s32[]{:S(2)}) async-start(s8[7340032]{0:T(1024)(128)(4,1)} %bitcast.32), calls=%async_computation.4 | async-start | bytes 6291456
  12.6 43.1 %collective-permute-start = (f32[3584,128]{1,0:T(8,128)S(1)}, f32[3584,128]{1,0:T(8,128)S(1)}, u32[]{:S(2)}, u32[]{:S(2)}) collective-permute-start(f32[3584,128]{1,0:T(8,128)S(1)} %fusion.5), channel_id=1, source_target_pairs={{0,4},{4,0},{8,12},{12,8},{16,20},{20,16},{24,28},{28,24},{1,5},{5... | collective-permute-start | bytes 5505032 | tf_op jit(solution)/shard_map/ppermute | solution.py:41
  55.9 44.0 %copy-start = (bf16[3584,128]{1,0:T(8,128)(2,1)S(1)}, bf16[3584,128]{1,0:T(8,128)(2,1)}, u32[]{:S(2)}) copy-start(bf16[3584,128]{1,0:T(8,128)(2,1)} %param.6) | copy-start | bytes 2752516
  55.9 41.2 %collective-permute-start.1 = (f32[3584,128]{1,0:T(8,128)S(1)}, f32[3584,128]{1,0:T(8,128)S(1)}, u32[]{:S(2)}, u32[]{:S(2)}) collective-permute-start(f32[3584,128]{1,0:T(8,128)S(1)} %add.93), channel_id=1, source_target_pairs={{0,8},{4,12},{8,0},{12,4},{16,24},{20,28},{24,16},{28,20},{1,9},{5... | collective-permute-start | bytes 5505032 | tf_op jit(solution)/shard_map/ppermute | solution.py:41
  97.4 80.6 %collective-permute-start.2 = (f32[3584,128]{1,0:T(8,128)S(1)}, f32[3584,128]{1,0:T(8,128)S(1)}, u32[]{:S(2)}, u32[]{:S(2)}) collective-permute-start(f32[3584,128]{1,0:T(8,128)S(1)} %add.94), channel_id=1, source_target_pairs={{0,16},{4,20},{8,24},{12,28},{16,0},{20,4},{24,8},{28,12},{1,17},{... | collective-permute-start | bytes 5505032 | tf_op jit(solution)/shard_map/ppermute | solution.py:41
  180.3 4.7 copy-start.4
  180.3 12.8 %copy-start.6 = (s32[2,1024]{1,0:T(2,128)S(1)}, s32[2,1024]{1,0:T(2,128)}, u32[]{:S(2)}) copy-start(s32[2,1024]{1,0:T(2,128)} %param.8) | copy-start | bytes 24580
  180.3 253.8 %all-reduce.7.cloned.1.call-start = ((), (), s32[]{:S(2)}) async-start(), calls=%async_computation | async-start | bytes 1048576 | tf_op jit(solution)/shard_map/psum | solution.py:54
  249.5 37.5 %collective-permute-start.3 = (f32[3584,128]{1,0:T(8,128)S(1)}, f32[3584,128]{1,0:T(8,128)S(1)}, u32[]{:S(2)}, u32[]{:S(2)}) collective-permute-start(f32[3584,128]{1,0:T(8,128)S(1)} %convolution_bitcast_fusion.1), channel_id=1, source_target_pairs={{0,4},{4,0},{8,12},{12,8},{16,20},{20,16},{24,28},{28,24},{1,5},{5... | collective-permute-start | bytes 5505032 | tf_op jit(solution)/shard_map/ppermute | solution.py:41
  287.0 113.4 %slice-start.2 = ((s8[7340032]{0:T(1024)(128)(4,1)}), s8[4194304]{0:T(1024)(128)(4,1)S(1)}, s32[]{:S(2)}) async-start(s8[7340032]{0:T(1024)(128)(4,1)} %bitcast.34), calls=%async_computation.5 | async-start | bytes 8388608
  287.2 113.2 %slice-start.3 = ((s8[7340032]{0:T(1024)(128)(4,1)}), s8[3145728]{0:T(1024)(128)(4,1)S(1)}, s32[]{:S(2)}) async-start(s8[7340032]{0:T(1024)(128)(4,1)} %bitcast.34), calls=%async_computation.6 | async-start | bytes 6291456
  287.2 37.8 %collective-permute-start.4 = (f32[3584,128]{1,0:T(8,128)S(1)}, f32[3584,128]{1,0:T(8,128)S(1)}, u32[]{:S(2)}, u32[]{:S(2)}) collective-permute-start(f32[3584,128]{1,0:T(8,128)S(1)} %add.97), channel_id=1, source_target_pairs={{0,8},{4,12},{8,0},{12,4},{16,24},{20,28},{24,16},{28,20},{1,9},{5... | collective-permute-start | bytes 5505032 | tf_op jit(solution)/shard_map/ppermute | solution.py:41
  325.2 74.9 %collective-permute-start.5 = (f32[3584,128]{1,0:T(8,128)S(1)}, f32[3584,128]{1,0:T(8,128)S(1)}, u32[]{:S(2)}, u32[]{:S(2)}) collective-permute-start(f32[3584,128]{1,0:T(8,128)S(1)} %add.98), channel_id=1, source_target_pairs={{0,16},{4,20},{8,24},{12,28},{16,0},{20,4},{24,8},{28,12},{1,17},{... | collective-permute-start | bytes 5505032 | tf_op jit(solution)/shard_map/ppermute | solution.py:41
  402.4 263.8 %all-reduce.9.cloned.1.call-start = ((), (), s32[]{:S(2)}) async-start(), calls=%async_computation.1 | async-start | bytes 1048576 | tf_op jit(solution)/shard_map/psum | solution.py:54
  437.2 5.5 copy-start.2
  442.6 40.6 %collective-permute-start.6 = (f32[3584,128]{1,0:T(8,128)S(1)}, f32[3584,128]{1,0:T(8,128)S(1)}, u32[]{:S(2)}, u32[]{:S(2)}) collective-permute-start(f32[3584,128]{1,0:T(8,128)S(1)} %convolution_bitcast_fusion), channel_id=1, source_target_pairs={{0,4},{4,0},{8,12},{12,8},{16,20},{20,16},{24,28},{28,24},{1,5},{5... | collective-permute-start | bytes 5505032 | tf_op jit(solution)/shard_map/ppermute | solution.py:41
  483.5 44.1 %copy-start.5 = (f32[1024,128]{1,0:T(8,128)S(1)}, f32[1024,128]{1,0:T(8,128)}, u32[]{:S(2)}) copy-start(f32[1024,128]{1,0:T(8,128)} %param.7) | copy-start | bytes 1572868
  483.5 40.0 %collective-permute-start.7 = (f32[3584,128]{1,0:T(8,128)S(1)}, f32[3584,128]{1,0:T(8,128)S(1)}, u32[]{:S(2)}, u32[]{:S(2)}) collective-permute-start(f32[3584,128]{1,0:T(8,128)S(1)} %add.101), channel_id=1, source_target_pairs={{0,8},{4,12},{8,0},{12,4},{16,24},{20,28},{24,16},{28,20},{1,9},{5... | collective-permute-start | bytes 5505032 | tf_op jit(solution)/shard_map/ppermute | solution.py:41
  524.9 79.7 %collective-permute-start.8 = (f32[3584,128]{1,0:T(8,128)}, f32[3584,128]{1,0:T(8,128)}, u32[]{:S(2)}, u32[]{:S(2)}) collective-permute-start(f32[3584,128]{1,0:T(8,128)} %add.102), channel_id=1, source_target_pairs={{0,16},{4,20},{8,24},{12,28},{16,0},{20,4},{24,8},{28,12},{1,17},{... | collective-permute-start | bytes 5505032 | tf_op jit(solution)/shard_map/ppermute | solution.py:41
  606.9 0.9 copy-start.1
  607.8 5.8 copy-start.3
Sparse Core Ops, SparseCore 0:
  180.4 37.1 all-reduce.10
  402.5 31.5 all-reduce.6
  613.1 34.9 all-reduce.8
